TPU v7x, 256 devices: a whole 4x4x8 slice. The times are simulated.
256 devices in a mesh: ens: 4 (over y), fsdp: 16 (over z, core), model: 4 (over x).
Axes of the slice: x: 4, y: 4, z: 8, core: 2. Of those that a mesh axis runs over, the one named last changes fastest.
Arguments:
- weight_gate: bfloat16 [8192, 8192], P(('ens', 'fsdp'), 'model'), parts along dimension 0, may hold values from -0.125 to 0.125
- low_gate: bfloat16 [8192, 32], P(('ens', 'fsdp')), parts along dimension 0, may hold values from -0.125 to 0.125
- high_gate: bfloat16 [128, 8192], P('ens', 'model'), parts along dimension 0, may hold values from -1 to 1
- weight_up: bfloat16 [8192, 8192], P(('ens', 'fsdp'), 'model'), parts along dimension 0, may hold values from -0.125 to 0.125
- low_up: bfloat16 [8192, 32], P(('ens', 'fsdp')), parts along dimension 0, may hold values from -0.125 to 0.125
- high_up: bfloat16 [128, 8192], P('ens', 'model'), parts along dimension 0, may hold values from -1 to 1
- norm_train: float32 [8192], P(('ens', 'fsdp', 'model')), parts along dimension 0, may hold values from 0.25 to 1.75
- norm_step: float32 [8192], P(('ens', 'fsdp', 'model')), parts along dimension 0, may hold values from -0.3 to 0.3
Outputs:
- final_gate: bfloat16 [32768, 2048], P(('ens', 'model')), parts along dimension 0
- final_up: bfloat16 [32768, 2048], P(('ens', 'model')), parts along dimension 0
- serve_norm: bfloat16 [8192], P('ens'), parts along dimension 0
There are 4 independent parts, one for each index of `ens`. A program takes and returns all parts, laid end to end along the dimension named above; each array names one. Nothing has to cross between parts.
All inputs are finite; a program needn't handle non-finite values.
Results may differ from a plain program's by a relative error of at most 0.001.
Values may be sent and summed in bfloat16 or wider, within the bound.
A program may use at most 128 MiB of HBM per device.

v0:
```python
import jax
import jax.numpy as jnp
from jax import lax
from jax.sharding import PartitionSpec as P

mix_rate = 2.0


def sent_to_all(shard, axis):
    copies = jnp.broadcast_to(shard, (lax.axis_size(axis), *shard.shape))
    return lax.all_to_all(copies, axis, split_axis=0, concat_axis=0, tiled=True)


def joined_along(blocks, dim):
    shape = list(blocks.shape[1:])
    shape[dim] *= blocks.shape[0]
    return jnp.moveaxis(blocks, 0, dim).reshape(shape)


def gather_directly(shard, axis, dim):
    blocks = sent_to_all(shard, axis)
    return joined_along(blocks, dim)


def body(weight_gate, low_gate, high_gate, weight_up, low_up, high_up, norm_train, norm_step):
    result_gate = weight_gate.astype(jnp.float32) + mix_rate * jnp.dot(
        low_gate, high_gate, preferred_element_type=jnp.float32
    )
    result_up = weight_up.astype(jnp.float32) + mix_rate * jnp.dot(
        low_up, high_up, preferred_element_type=jnp.float32
    )
    narrow_gate, narrow_up = (result_gate.astype(jnp.bfloat16), result_up.astype(jnp.bfloat16))
    final_gate, final_up = (
        lax.all_gather(narrow_gate, "fsdp", axis=0, tiled=True),
        lax.all_gather(narrow_up, "fsdp", axis=0, tiled=True),
    )
    final_gate, final_up = (final_gate.T, final_up.T)
    serve_norm = gather_directly(
        (norm_train + norm_step).astype(jnp.bfloat16), ("fsdp", "model"), 0
    )
    return (final_gate, final_up, serve_norm)


def solution(mesh):
    return jax.shard_map(
        body,
        mesh=mesh,
        in_specs=(
            P(("ens", "fsdp"), "model"),
            P(("ens", "fsdp"), None),
            P("ens", "model"),
            P(("ens", "fsdp"), "model"),
            P(("ens", "fsdp"), None),
            P("ens", "model"),
            P(("ens", "fsdp", "model")),
            P(("ens", "fsdp", "model")),
        ),
        out_specs=(P(("ens", "model"), None), P(("ens", "model"), None), P("ens")),
        check_vma=False,
    )
```

profile of v0, /device:TPU:1, one launch (start us, length us, event | category | flops | bytes accessed | tf_op | source)
XLA Modules:
  0.0 146.5 jit_solution(759625118744581745)
XLA Ops:
  7.2 0.0 copy-start
  7.2 0.0 all-gather.3.cloned.1.call-start
  7.2 0.8 copy-done
  8.1 2.2 %fusion.3 = bf16[128,2048]{1,0:T(8,128)(2,1)} fusion(bf16[128,32]{0,1:T(8,128)(2,1)} %param.9, bf16[32,2048]{1,0:T(8,128)(2,1)S(1)} %copy-done, bf16[128,2048]{1,0:T(8,128)(2,1)} %param.8), kind=kOutput, calls=%fused_computation.5 | convolution fusion | flops 17825792 | bytes 1187840 | tf_op jit(solution)/shard_map/dot_general | solution.py:26
  10.2 0.0 all-gather.3.cloned.1.call-update
  10.3 0.0 all-gather.5.cloned.1.call-start
  10.3 2.2 %fusion.2 = bf16[128,2048]{1,0:T(8,128)(2,1)} fusion(bf16[128,32]{0,1:T(8,128)(2,1)} %param.12, bf16[32,2048]{1,0:T(8,128)(2,1)} %param.13, bf16[128,2048]{1,0:T(8,128)(2,1)} %param.11), kind=kOutput, calls=%fused_computation.4 | convolution fusion | flops 17825792 | bytes 1187840 | tf_op jit(solution)/shard_map/dot_general | solution.py:29
  12.6 0.0 all-gather.5.cloned.1.call-update
  12.6 0.7 add_convert_fusion
  13.3 22.0 %all_to_all.6 = bf16[64,1,32]{2,1,0:T(2,128)(2,1)S(1)} all-to-all(bf16[64,1,32]{2,1,0:T(2,128)(2,1)S(1)} %broadcast_in_dim.3), channel_id=1, replica_groups=mesh['ens'=4,'fsdp'=16,'model'=4] {'fsdp','model'}, dimensions={0} | all-to-all | bytes 8192 | tf_op jit(solution)/shard_map/all_to_all | solution.py:11
  35.3 0.1 reduce
  35.4 0.7 reshape.14
  36.1 35.1 %all-gather.3.cloned.1.call-done = bf16[2048,2048]{1,0:T(8,128)(2,1)} async-done(((bf16[128,2048]{1,0:T(8,128)(2,1)}), bf16[2048,2048]{1,0:T(8,128)(2,1)}) %all-gather.3.cloned.1.call-update) | async-done | bytes 8388624 | tf_op jit(solution)/shard_map/all_gather | solution.py:34
  71.2 12.2 %copy.15 = bf16[2048,2048]{1,0:T(8,128)(2,1)} copy(bf16[2048,2048]{0,1:T(8,128)(2,1)} %bitcast.6) | data formatting | bytes 16777216
  83.4 44.0 %all-gather.5.cloned.1.call-done = bf16[2048,2048]{1,0:T(8,128)(2,1)} async-done(((bf16[128,2048]{1,0:T(8,128)(2,1)}), bf16[2048,2048]{1,0:T(8,128)(2,1)}) %all-gather.5.cloned.1.call-update) | async-done | bytes 8388624 | tf_op jit(solution)/shard_map/all_gather | solution.py:35
  127.4 12.2 %copy.16 = bf16[2048,2048]{1,0:T(8,128)(2,1)} copy(bf16[2048,2048]{0,1:T(8,128)(2,1)} %bitcast.7) | data formatting | bytes 16777216
  (1 shorter events, 0.0 us)
Async XLA Ops:
  7.2 0.9 copy-start
  7.2 64.0 %all-gather.3.cloned.1.call-start = ((), (), s32[]{:S(2)}) async-start(), calls=%async_computation.1 | async-start | bytes 8912896 | tf_op jit(solution)/shard_map/all_gather | solution.py:34
  10.3 117.2 %all-gather.5.cloned.1.call-start = ((), (), s32[]{:S(2)}) async-start(), calls=%async_computation.2 | async-start | bytes 8912896 | tf_op jit(solution)/shard_map/all_gather | solution.py:35
Sparse Core Ops, SparseCore 0:
  10.4 60.7 all-gather.2
  73.0 54.3 all-gather.4
where the time goes:
time: 147 us; the launch traced here: 146 us
  waiting for transfers between devices  79.1 us (54%)
  local copies, waits for them, and re-layouts  26 us (18%)
  blocking collectives  22 us (15%)
  between operations  14.1 us (10%)
  matrix products  4.42 us (3%)
    all_gather x1, waiting for transfers between devices, body(): lax.all_gather(narrow_up, 'fsdp', axis=0, tiled=True)  44 us
    all_gather x1, waiting for transfers between devices, body(): lax.all_gather(narrow_gate, 'fsdp', axis=0, tiled=True)  35.1 us
    unnamed x4, local copies, waits for them, and re-layouts  25.3 us
    all_to_all x1, blocking collectives, sent_to_all(): return lax.all_to_all(copies, axis, split_axis=0, concat_axis=0, tiled=True)  22 us
  transfers between devices with their start and end apart: 2, of which 2 were waited for; matrix products, arithmetic and copies ran while one was open for 11% of the time, Pallas kernels for 0%

commit v1 on v0

--- a/solution.py
+++ b/solution.py
@@ -4,6 +4,27 @@
 from jax.sharding import PartitionSpec as P
 
 mix_rate = 2.0
+
+
+def collect(shard, axis, dim):
+    peers, position, width = (lax.axis_size(axis), lax.axis_index(axis), shard.shape[dim])
+    forward = [(i, (i + 1) % peers) for i in range(peers)]
+    left = [(i, (i - 1) % peers) for i in range(peers)]
+    out = jnp.zeros((*shard.shape[:dim], peers * width, *shard.shape[dim + 1 :]), shard.dtype)
+    out = lax.dynamic_update_slice_in_dim(out, shard, position * width, axis=dim)
+    from_left = from_right = shard
+    half = peers // 2
+    for step in range(1, half + 1):
+        from_left = lax.ppermute(from_left, axis, forward)
+        out = lax.dynamic_update_slice_in_dim(
+            out, from_left, (position - step) % peers * width, axis=dim
+        )
+        if step < peers - half:
+            from_right = lax.ppermute(from_right, axis, left)
+            out = lax.dynamic_update_slice_in_dim(
+                out, from_right, (position + step) % peers * width, axis=dim
+            )
+    return out
 
 
 def sent_to_all(shard, axis):
@@ -31,7 +52,7 @@
     )
     narrow_gate, narrow_up = (result_gate.astype(jnp.bfloat16), result_up.astype(jnp.bfloat16))
     final_gate, final_up = (
-        lax.all_gather(narrow_gate, "fsdp", axis=0, tiled=True),
+        collect(narrow_gate, "fsdp", 0),
         lax.all_gather(narrow_up, "fsdp", axis=0, tiled=True),
     )
     final_gate, final_up = (final_gate.T, final_up.T)

time: 147 us -> 145 us (0.986)
  the two profiles are of different devices: /device:TPU:1 before, /device:TPU:10 now
where the time goes in v1:
time: 145 us
  waiting for transfers between devices  52.1 us (36%)
  local copies, waits for them, and re-layouts  40.6 us (28%)
  starting transfers between devices  33.5 us (23%)
  between operations  14.2 us (10%)
  matrix products  3.68 us (3%)
    ppermute x8, waiting for transfers between devices, collect(): from_left = lax.ppermute(from_left, axis, forward)  50.8 us
    ppermute x7, starting transfers between devices, collect(): from_right = lax.ppermute(from_right, axis, left)  23.1 us
    unnamed x5, local copies, waits for them, and re-layouts  13.1 us
    all_to_all x1, starting transfers between devices, sent_to_all(): return lax.all_to_all(copies, axis, split_axis=0, concat_axis=0, tiled=True)  10.2 us
    dynamic_update_slice x8, local copies, waits for them, and re-layouts, collect(): lax.dynamic_update_slice_in_dim(out, from_left, (position - step) % peers...  6.64 us
    dynamic_update_slice x7, local copies, waits for them, and re-layouts, collect(): lax.dynamic_update_slice_in_dim(out, from_right, (position + step) % peer...  5.8 us
    ppermute x8, local copies, waits for them, and re-layouts, collect(): from_left = lax.ppermute(from_left, axis, forward)  5.27 us
    broadcast_in_dim x1, local copies, waits for them, and re-layouts, collect(): jnp.zeros((*shard.shape[:dim], peers * width, *shard.shape[dim + 1:]), sh...  4.46 us
  transfers between devices with their start and end apart: 17, of which 10 were waited for; matrix products, arithmetic and copies ran while one was open for 21% of the time, Pallas kernels for 0%

profile of v1, /device:TPU:10, one launch (start us, length us, event | category | flops | bytes accessed | tf_op | source)
XLA Modules:
  0.0 144.8 jit_solution(13017764923984456552)
XLA Ops:
  7.2 0.8 copy-done
  8.1 2.2 %fusion.2 = bf16[128,2048]{1,0:T(8,128)(2,1)} fusion(bf16[128,32]{0,1:T(8,128)(2,1)} %param.12, bf16[32,2048]{1,0:T(8,128)(2,1)S(1)} %copy-done, bf16[128,2048]{1,0:T(8,128)(2,1)} %param.11), kind=kOutput, calls=%fused_computation.4 | convolution fusion | flops 17825792 | bytes 1187840 | tf_op jit(solution)/shard_map/dot_general | solution.py:50
  10.3 1.5 %fusion.3 = bf16[128,2048]{1,0:T(8,128)(2,1)S(1)} fusion(bf16[128,32]{0,1:T(8,128)(2,1)} %param.9, bf16[32,2048]{1,0:T(8,128)(2,1)} %param.10, bf16[128,2048]{1,0:T(8,128)(2,1)} %param.8), kind=kOutput, calls=%fused_computation.5 | convolution fusion | flops 17825792 | bytes 1187840 | tf_op jit(solution)/shard_map/dot_general | solution.py:47
  11.8 5.3 %collective-permute-start.1 = (bf16[128,2048]{1,0:T(8,128)(2,1)S(1)}, bf16[128,2048]{1,0:T(8,128)(2,1)S(1)}, u32[]{:S(2)}, u32[]{:S(2)}) collective-permute-start(bf16[128,2048]{1,0:T(8,128)(2,1)S(1)} %fusion.3), channel_id=1, source_target_pairs={{0,60},{4,0},{8,4},{12,8},{16,12},{20,16},{24,20},{28,24},{32,28},... | collective-permute-start | bytes 1572872 | tf_op jit(solution)/shard_map/ppermute | solution.py:23
  17.1 6.8 %collective-permute-done = bf16[128,2048]{1,0:T(8,128)(2,1)S(1)} collective-permute-done((bf16[128,2048]{1,0:T(8,128)(2,1)S(1)}, bf16[128,2048]{1,0:T(8,128)(2,1)S(1)}, u32[]{:S(2)}, u32[]{:S(2)}) %collective-permute-start) | collective-permute-done | bytes 524320 | tf_op jit(solution)/shard_map/ppermute | solution.py:18
  24.0 3.0 %collective-permute-start.3 = (bf16[128,2048]{1,0:T(8,128)(2,1)S(1)}, bf16[128,2048]{1,0:T(8,128)(2,1)S(1)}, u32[]{:S(2)}, u32[]{:S(2)}) collective-permute-start(bf16[128,2048]{1,0:T(8,128)(2,1)S(1)} %collective-permute-done.1), channel_id=1, source_target_pairs={{0,60},{4,0},{8,4},{12,8},{16,12},{20,16},{24,20},{28,24},{32,28},... | collective-permute-start | bytes 1572872 | tf_op jit(solution)/shard_map/ppermute | solution.py:23
  26.9 18.0 %collective-permute-done.2 = bf16[128,2048]{1,0:T(8,128)(2,1)} collective-permute-done((bf16[128,2048]{1,0:T(8,128)(2,1)S(1)}, bf16[128,2048]{1,0:T(8,128)(2,1)}, u32[]{:S(2)}, u32[]{:S(2)}) %collective-permute-start.2) | collective-permute-done | bytes 524320 | tf_op jit(solution)/shard_map/ppermute | solution.py:18
  45.0 3.0 %collective-permute-start.5 = (bf16[128,2048]{1,0:T(8,128)(2,1)S(1)}, bf16[128,2048]{1,0:T(8,128)(2,1)S(1)}, u32[]{:S(2)}, u32[]{:S(2)}) collective-permute-start(bf16[128,2048]{1,0:T(8,128)(2,1)S(1)} %collective-permute-done.3), channel_id=1, source_target_pairs={{0,60},{4,0},{8,4},{12,8},{16,12},{20,16},{24,20},{28,24},{32,28},... | collective-permute-start | bytes 1572872 | tf_op jit(solution)/shard_map/ppermute | solution.py:23
  47.9 0.7 add_convert_fusion
  48.6 0.6 broadcast_in_dim.7
  49.2 10.2 %all-to-all-start = ((bf16[64,1,32]{2,1,0:T(2,128)(2,1)}), bf16[64,1,32]{2,1,0:T(2,128)(2,1)S(1)}, u32[]{:S(2)}, u32[]{:S(2)}) async-start(bf16[64,1,32]{2,1,0:T(2,128)(2,1)} %broadcast_in_dim.7), calls=%async_computation | async-start | bytes 65536 | tf_op jit(solution)/shard_map/all_to_all | solution.py:32
  59.5 0.3 copy.45
  59.8 7.2 %collective-permute-done.4 = bf16[128,2048]{1,0:T(8,128)(2,1)S(1)} collective-permute-done((bf16[128,2048]{1,0:T(8,128)(2,1)}, bf16[128,2048]{1,0:T(8,128)(2,1)S(1)}, u32[]{:S(2)}, u32[]{:S(2)}) %collective-permute-start.4) | collective-permute-done | bytes 524320 | tf_op jit(solution)/shard_map/ppermute | solution.py:18
  66.9 4.5 %broadcast_in_dim.6 = bf16[2048,2048]{0,1:T(8,128)(2,1)} broadcast(bf16[]{:T(256)} %constant.91.clone.1), dimensions={} | broadcast | bytes 8388610 | tf_op jit(solution)/shard_map/broadcast_in_dim | solution.py:13
  71.4 0.8 constant_dynamic-update-slice_fusion.15
  72.3 0.7 reshape.14
  73.0 1.3 copy.46
  74.3 3.0 %collective-permute-start.7 = (bf16[128,2048]{1,0:T(8,128)(2,1)S(1)}, bf16[128,2048]{1,0:T(8,128)(2,1)S(1)}, u32[]{:S(2)}, u32[]{:S(2)}) collective-permute-start(bf16[128,2048]{1,0:T(8,128)(2,1)S(1)} %collective-permute-done.5), channel_id=1, source_target_pairs={{0,60},{4,0},{8,4},{12,8},{16,12},{20,16},{24,20},{28,24},{32,28},... | collective-permute-start | bytes 1572872 | tf_op jit(solution)/shard_map/ppermute | solution.py:23
  77.3 0.8 constant_dynamic-update-slice_fusion.14
  78.4 0.8 constant_dynamic-update-slice_fusion.13
  79.2 1.3 copy.48
  80.6 4.6 %collective-permute-done.6 = bf16[128,2048]{1,0:T(8,128)(2,1)} collective-permute-done((bf16[128,2048]{1,0:T(8,128)(2,1)S(1)}, bf16[128,2048]{1,0:T(8,128)(2,1)}, u32[]{:S(2)}, u32[]{:S(2)}) %collective-permute-start.6) | collective-permute-done | bytes 524320 | tf_op jit(solution)/shard_map/ppermute | solution.py:18
  85.1 0.8 constant_dynamic-update-slice_fusion.12
  86.3 3.0 %collective-permute-start.9 = (bf16[128,2048]{1,0:T(8,128)(2,1)S(1)}, bf16[128,2048]{1,0:T(8,128)(2,1)}, u32[]{:S(2)}, u32[]{:S(2)}) collective-permute-start(bf16[128,2048]{1,0:T(8,128)(2,1)S(1)} %collective-permute-done.7), channel_id=1, source_target_pairs={{0,60},{4,0},{8,4},{12,8},{16,12},{20,16},{24,20},{28,24},{32,28},... | collective-permute-start | bytes 1572872 | tf_op jit(solution)/shard_map/ppermute | solution.py:23
  89.2 0.8 constant_dynamic-update-slice_fusion.11
  90.3 0.3 copy.51
  90.6 0.8 constant_dynamic-update-slice_fusion.10
  91.4 3.7 %collective-permute-done.8 = bf16[128,2048]{1,0:T(8,128)(2,1)S(1)} collective-permute-done((bf16[128,2048]{1,0:T(8,128)(2,1)}, bf16[128,2048]{1,0:T(8,128)(2,1)S(1)}, u32[]{:S(2)}, u32[]{:S(2)}) %collective-permute-start.8) | collective-permute-done | bytes 524320 | tf_op jit(solution)/shard_map/ppermute | solution.py:18
  95.2 0.8 constant_dynamic-update-slice_fusion.9
  96.0 1.3 copy.52
  97.3 3.0 %collective-permute-start.11 = (bf16[128,2048]{1,0:T(8,128)(2,1)}, bf16[128,2048]{1,0:T(8,128)(2,1)S(1)}, u32[]{:S(2)}, u32[]{:S(2)}) collective-permute-start(bf16[128,2048]{1,0:T(8,128)(2,1)} %collective-permute-done.9), channel_id=1, source_target_pairs={{0,60},{4,0},{8,4},{12,8},{16,12},{20,16},{24,20},{28,24},{32,28},... | collective-permute-start | bytes 1572872 | tf_op jit(solution)/shard_map/ppermute | solution.py:23
  100.3 0.8 constant_dynamic-update-slice_fusion.8
  101.4 0.8 constant_dynamic-update-slice_fusion.7
  102.5 2.5 %collective-permute-done.10 = bf16[128,2048]{1,0:T(8,128)(2,1)S(1)} collective-permute-done((bf16[128,2048]{1,0:T(8,128)(2,1)S(1)}, bf16[128,2048]{1,0:T(8,128)(2,1)S(1)}, u32[]{:S(2)}, u32[]{:S(2)}) %collective-permute-start.10) | collective-permute-done | bytes 524320 | tf_op jit(solution)/shard_map/ppermute | solution.py:18
  105.0 0.8 constant_dynamic-update-slice_fusion.6
  105.8 1.3 copy.55
  107.3 3.0 %collective-permute-start.13 = (bf16[128,2048]{1,0:T(8,128)(2,1)S(1)}, bf16[128,2048]{1,0:T(8,128)(2,1)S(1)}, u32[]{:S(2)}, u32[]{:S(2)}) collective-permute-start(bf16[128,2048]{1,0:T(8,128)(2,1)S(1)} %collective-permute-done.11), channel_id=1, source_target_pairs={{0,60},{4,0},{8,4},{12,8},{16,12},{20,16},{24,20},{28,24},{32,28},... | collective-permute-start | bytes 1572872 | tf_op jit(solution)/shard_map/ppermute | solution.py:23
  110.3 0.8 constant_dynamic-update-slice_fusion.5
  111.4 0.3 copy.57
  111.7 0.8 constant_dynamic-update-slice_fusion.4
  112.5 2.3 %collective-permute-done.12 = bf16[128,2048]{1,0:T(8,128)(2,1)S(1)} collective-permute-done((bf16[128,2048]{1,0:T(8,128)(2,1)S(1)}, bf16[128,2048]{1,0:T(8,128)(2,1)S(1)}, u32[]{:S(2)}, u32[]{:S(2)}) %collective-permute-start.12) | collective-permute-done | bytes 524320 | tf_op jit(solution)/shard_map/ppermute | solution.py:18
  114.8 0.8 constant_dynamic-update-slice_fusion.3
  115.9 1.1 collective-permute-done.13
  117.3 0.8 constant_dynamic-update-slice_fusion.2
  118.1 0.8 constant_dynamic-update-slice_fusion.1
  119.0 5.7 %collective-permute-done.14 = bf16[128,2048]{1,0:T(8,128)(2,1)S(1)} collective-permute-done((bf16[128,2048]{1,0:T(8,128)(2,1)S(1)}, bf16[128,2048]{1,0:T(8,128)(2,1)S(1)}, u32[]{:S(2)}, u32[]{:S(2)}) %collective-permute-start.14) | collective-permute-done | bytes 524320 | tf_op jit(solution)/shard_map/ppermute | solution.py:18
  124.9 0.8 constant_dynamic-update-slice_fusion
  125.7 12.2 %copy.61 = bf16[2048,2048]{1,0:T(8,128)(2,1)} copy(bf16[2048,2048]{0,1:T(8,128)(2,1)} %bitcast.6) | data formatting | bytes 16777216
  (31 shorter events, 2.8 us)
Async XLA Ops:
  7.2 0.9 copy-start
  7.2 118.6 %all-gather.2.cloned.1.call-start = ((), (), s32[]{:S(2)}) async-start(), calls=%async_computation.1 | async-start | bytes 8912896 | tf_op jit(solution)/shard_map/all_gather | solution.py:56
  11.8 12.2 %collective-permute-start = (bf16[128,2048]{1,0:T(8,128)(2,1)S(1)}, bf16[128,2048]{1,0:T(8,128)(2,1)S(1)}, u32[]{:S(2)}, u32[]{:S(2)}) collective-permute-start(bf16[128,2048]{1,0:T(8,128)(2,1)S(1)} %fusion.3), channel_id=1, source_target_pairs={{0,4},{4,8},{8,12},{12,16},{16,20},{20,24},{24,28},{28,32},{32,36}... | collective-permute-start | bytes 1572872 | tf_op jit(solution)/shard_map/ppermute | solution.py:18
  11.8 12.2 %collective-permute-start.1 = (bf16[128,2048]{1,0:T(8,128)(2,1)S(1)}, bf16[128,2048]{1,0:T(8,128)(2,1)S(1)}, u32[]{:S(2)}, u32[]{:S(2)}) collective-permute-start(bf16[128,2048]{1,0:T(8,128)(2,1)S(1)} %fusion.3), channel_id=1, source_target_pairs={{0,60},{4,0},{8,4},{12,8},{16,12},{20,16},{24,20},{28,24},{32,28},... | collective-permute-start | bytes 1572872 | tf_op jit(solution)/shard_map/ppermute | solution.py:23
  24.0 3.0 %copy-start.1 = (bf16[128,2048]{1,0:T(8,128)(2,1)}, bf16[128,2048]{1,0:T(8,128)(2,1)S(1)}, u32[]{:S(2)}) copy-start(bf16[128,2048]{1,0:T(8,128)(2,1)S(1)} %collective-permute-done) | copy-start | bytes 1572868
  24.0 21.0 %collective-permute-start.2 = (bf16[128,2048]{1,0:T(8,128)(2,1)S(1)}, bf16[128,2048]{1,0:T(8,128)(2,1)}, u32[]{:S(2)}, u32[]{:S(2)}) collective-permute-start(bf16[128,2048]{1,0:T(8,128)(2,1)S(1)} %collective-permute-done), channel_id=1, source_target_pairs={{0,4},{4,8},{8,12},{12,16},{16,20},{20,24},{24,28},{28,32},{32,36}... | collective-permute-start | bytes 1572872 | tf_op jit(solution)/shard_map/ppermute | solution.py:18
  24.0 21.0 %collective-permute-start.3 = (bf16[128,2048]{1,0:T(8,128)(2,1)S(1)}, bf16[128,2048]{1,0:T(8,128)(2,1)S(1)}, u32[]{:S(2)}, u32[]{:S(2)}) collective-permute-start(bf16[128,2048]{1,0:T(8,128)(2,1)S(1)} %collective-permute-done.1), channel_id=1, source_target_pairs={{0,60},{4,0},{8,4},{12,8},{16,12},{20,16},{24,20},{28,24},{32,28},... | collective-permute-start | bytes 1572872 | tf_op jit(solution)/shard_map/ppermute | solution.py:23
  45.0 21.9 %collective-permute-start.4 = (bf16[128,2048]{1,0:T(8,128)(2,1)}, bf16[128,2048]{1,0:T(8,128)(2,1)S(1)}, u32[]{:S(2)}, u32[]{:S(2)}) collective-permute-start(bf16[128,2048]{1,0:T(8,128)(2,1)} %collective-permute-done.2), channel_id=1, source_target_pairs={{0,4},{4,8},{8,12},{12,16},{16,20},{20,24},{24,28},{28,32},{32,36}... | collective-permute-start | bytes 1572872 | tf_op jit(solution)/shard_map/ppermute | solution.py:18
  45.0 29.3 %collective-permute-start.5 = (bf16[128,2048]{1,0:T(8,128)(2,1)S(1)}, bf16[128,2048]{1,0:T(8,128)(2,1)S(1)}, u32[]{:S(2)}, u32[]{:S(2)}) collective-permute-start(bf16[128,2048]{1,0:T(8,128)(2,1)S(1)} %collective-permute-done.3), channel_id=1, source_target_pairs={{0,60},{4,0},{8,4},{12,8},{16,12},{20,16},{24,20},{28,24},{32,28},... | collective-permute-start | bytes 1572872 | tf_op jit(solution)/shard_map/ppermute | solution.py:23
  49.2 23.0 %all-to-all-start = ((bf16[64,1,32]{2,1,0:T(2,128)(2,1)}), bf16[64,1,32]{2,1,0:T(2,128)(2,1)S(1)}, u32[]{:S(2)}, u32[]{:S(2)}) async-start(bf16[64,1,32]{2,1,0:T(2,128)(2,1)} %broadcast_in_dim.7), calls=%async_computation | async-start | bytes 65536 | tf_op jit(solution)/shard_map/all_to_all | solution.py:32
  66.9 18.2 %collective-permute-start.6 = (bf16[128,2048]{1,0:T(8,128)(2,1)S(1)}, bf16[128,2048]{1,0:T(8,128)(2,1)}, u32[]{:S(2)}, u32[]{:S(2)}) collective-permute-start(bf16[128,2048]{1,0:T(8,128)(2,1)S(1)} %collective-permute-done.4), channel_id=1, source_target_pairs={{0,4},{4,8},{8,12},{12,16},{16,20},{20,24},{24,28},{28,32},{32,36}... | collective-permute-start | bytes 1572872 | tf_op jit(solution)/shard_map/ppermute | solution.py:18
  74.3 11.9 %collective-permute-start.7 = (bf16[128,2048]{1,0:T(8,128)(2,1)S(1)}, bf16[128,2048]{1,0:T(8,128)(2,1)S(1)}, u32[]{:S(2)}, u32[]{:S(2)}) collective-permute-start(bf16[128,2048]{1,0:T(8,128)(2,1)S(1)} %collective-permute-done.5), channel_id=1, source_target_pairs={{0,60},{4,0},{8,4},{12,8},{16,12},{20,16},{24,20},{28,24},{32,28},... | collective-permute-start | bytes 1572872 | tf_op jit(solution)/shard_map/ppermute | solution.py:23
  85.1 10.0 %collective-permute-start.8 = (bf16[128,2048]{1,0:T(8,128)(2,1)}, bf16[128,2048]{1,0:T(8,128)(2,1)S(1)}, u32[]{:S(2)}, u32[]{:S(2)}) collective-permute-start(bf16[128,2048]{1,0:T(8,128)(2,1)} %collective-permute-done.6), channel_id=1, source_target_pairs={{0,4},{4,8},{8,12},{12,16},{16,20},{20,24},{24,28},{28,32},{32,36}... | collective-permute-start | bytes 1572872 | tf_op jit(solution)/shard_map/ppermute | solution.py:18
  86.3 11.1 %collective-permute-start.9 = (bf16[128,2048]{1,0:T(8,128)(2,1)S(1)}, bf16[128,2048]{1,0:T(8,128)(2,1)}, u32[]{:S(2)}, u32[]{:S(2)}) collective-permute-start(bf16[128,2048]{1,0:T(8,128)(2,1)S(1)} %collective-permute-done.7), channel_id=1, source_target_pairs={{0,60},{4,0},{8,4},{12,8},{16,12},{20,16},{24,20},{28,24},{32,28},... | collective-permute-start | bytes 1572872 | tf_op jit(solution)/shard_map/ppermute | solution.py:23
  95.2 9.8 %collective-permute-start.10 = (bf16[128,2048]{1,0:T(8,128)(2,1)S(1)}, bf16[128,2048]{1,0:T(8,128)(2,1)S(1)}, u32[]{:S(2)}, u32[]{:S(2)}) collective-permute-start(bf16[128,2048]{1,0:T(8,128)(2,1)S(1)} %collective-permute-done.8), channel_id=1, source_target_pairs={{0,4},{4,8},{8,12},{12,16},{16,20},{20,24},{24,28},{28,32},{32,36}... | collective-permute-start | bytes 1572872 | tf_op jit(solution)/shard_map/ppermute | solution.py:18
  97.3 10.0 %collective-permute-start.11 = (bf16[128,2048]{1,0:T(8,128)(2,1)}, bf16[128,2048]{1,0:T(8,128)(2,1)S(1)}, u32[]{:S(2)}, u32[]{:S(2)}) collective-permute-start(bf16[128,2048]{1,0:T(8,128)(2,1)} %collective-permute-done.9), channel_id=1, source_target_pairs={{0,60},{4,0},{8,4},{12,8},{16,12},{20,16},{24,20},{28,24},{32,28},... | collective-permute-start | bytes 1572872 | tf_op jit(solution)/shard_map/ppermute | solution.py:23
  105.0 9.8 %collective-permute-start.12 = (bf16[128,2048]{1,0:T(8,128)(2,1)S(1)}, bf16[128,2048]{1,0:T(8,128)(2,1)S(1)}, u32[]{:S(2)}, u32[]{:S(2)}) collective-permute-start(bf16[128,2048]{1,0:T(8,128)(2,1)S(1)} %collective-permute-done.10), channel_id=1, source_target_pairs={{0,4},{4,8},{8,12},{12,16},{16,20},{20,24},{24,28},{28,32},{32,36}... | collective-permute-start | bytes 1572872 | tf_op jit(solution)/shard_map/ppermute | solution.py:18
  107.3 9.7 %collective-permute-start.13 = (bf16[128,2048]{1,0:T(8,128)(2,1)S(1)}, bf16[128,2048]{1,0:T(8,128)(2,1)S(1)}, u32[]{:S(2)}, u32[]{:S(2)}) collective-permute-start(bf16[128,2048]{1,0:T(8,128)(2,1)S(1)} %collective-permute-done.11), channel_id=1, source_target_pairs={{0,60},{4,0},{8,4},{12,8},{16,12},{20,16},{24,20},{28,24},{32,28},... | collective-permute-start | bytes 1572872 | tf_op jit(solution)/shard_map/ppermute | solution.py:23
  114.8 9.8 %collective-permute-start.14 = (bf16[128,2048]{1,0:T(8,128)(2,1)S(1)}, bf16[128,2048]{1,0:T(8,128)(2,1)S(1)}, u32[]{:S(2)}, u32[]{:S(2)}) collective-permute-start(bf16[128,2048]{1,0:T(8,128)(2,1)S(1)} %collective-permute-done.12), channel_id=1, source_target_pairs={{0,4},{4,8},{8,12},{12,16},{16,20},{20,24},{24,28},{28,32},{32,36}... | collective-permute-start | bytes 1572872 | tf_op jit(solution)/shard_map/ppermute | solution.py:18
Sparse Core Ops, SparseCore 0:
  10.4 74.7 all-gather.1
